TPU v7x, 256 devices: a whole 4x4x8 slice. The times are simulated.
256 devices in a mesh: grid: 32 (over y, x, core), rows: 8 (over z).
Axes of the slice: x: 4, y: 4, z: 8, core: 2. Of those that a mesh axis runs over, the one named last changes fastest.
Arguments:
- density: bfloat16 [32, 128, 4096], P(None, 'rows', 'grid'), as said below
- basis_values: bfloat16 [64, 16, 128, 512], P('grid', None, 'rows'), may hold values from -0.59765625 to 0.59765625
- grid_points: float32 [64, 3, 512], P('grid'), may hold values from -4 to 4
- grid_weights: float32 [64, 512], P('grid'), may hold values from 0.05 to 1
- screened_blocks: int32 [64, 16], P('grid'), may hold values from 0 to 31, as said below
Outputs:
- exchange: float32 [32, 128, 4096], P(None, 'rows', 'grid')
Inputs may be any that keep to these rules, and one draw needn't show every extreme that they name: density is symmetric: density[a, i, b * 128 + j] equals density[b, j, a * 128 + i]. `screened_blocks`: each row holds 16 distinct block numbers.
All inputs are finite; a program needn't handle non-finite values.
Results may differ from a plain program's by a relative error of at most 0.00055.
The roundings to bfloat16 on the way count: a program that leaves them out, or rounds other values in their place, can miss the bound.
Values may be sent and summed in bfloat16 or wider, within the bound.
A program may use at most 64 MiB of HBM per device.

v0:
```python
import jax
import jax.numpy as jnp
from jax import lax
from jax.sharding import PartitionSpec as P


def copy_for_each(shard, axis):
    copies = jnp.broadcast_to(shard, (lax.axis_size(axis), *shard.shape))
    return lax.all_to_all(copies, axis, split_axis=0, concat_axis=0, tiled=True)


def joined_along(blocks, dim):
    shape = list(blocks.shape[1:])
    shape[dim] *= blocks.shape[0]
    return jnp.moveaxis(blocks, 0, dim).reshape(shape)


def gather_directly(shard, axis, dim):
    blocks = copy_for_each(shard, axis)
    return joined_along(blocks, dim)


def body(density, basis_values, grid_points, grid_weights, screened_blocks):
    nblocks = density.shape[0]
    rows_mine = density.shape[1]
    block_size = rows_mine * lax.axis_size("rows")
    nbasis = nblocks * block_size
    nsig = basis_values.shape[1]
    npoints = basis_values.shape[3]
    stripe = lax.all_gather(density, "grid", axis=2, tiled=True)
    totals = jnp.zeros((nblocks, rows_mine, nblocks, block_size), jnp.float32)
    for batch_index in range(basis_values.shape[0]):
        blocks = screened_blocks[batch_index]
        row_pick = jnp.take(stripe, blocks, axis=0).reshape(nsig * rows_mine, nblocks, block_size)
        chosen = jnp.take(row_pick, blocks, axis=1)
        local_values = basis_values[batch_index]
        x_mine = local_values.reshape(nsig * rows_mine, npoints)
        fsum = jnp.einsum(
            "mtk,tkp->mp",
            chosen,
            gather_directly(local_values, "rows", 1),
            preferred_element_type=jnp.float32,
        )
        fmat = fsum.astype(jnp.bfloat16)
        intersection_part = lax.dot_general(
            x_mine, fmat, (((0,), (0,)), ((), ())), preferred_element_type=jnp.float32
        )
        intersection = lax.psum(intersection_part, "rows")
        places = grid_points[batch_index]
        weights = grid_weights[batch_index]
        diffs = places[:, :, None] - places[:, None, :]
        kern = 1.0 / jnp.sqrt(jnp.sum(diffs * diffs, axis=0) + 0.5)
        mixed = (weights[:, None] * kern * intersection).astype(jnp.bfloat16)
        potential = (
            jnp.dot(x_mine, mixed, preferred_element_type=jnp.float32) * weights[None, :]
        ).astype(jnp.bfloat16)
        potential = potential.reshape(nsig, rows_mine, npoints)
        block_k = jnp.einsum(
            "mp,tkp->mtk",
            x_mine,
            lax.all_gather(potential, "rows", axis=1, tiled=True),
            preferred_element_type=jnp.float32,
        )
        block_k = block_k.reshape(nsig, rows_mine, nsig, block_size)
        totals = totals.at[blocks[:, None], :, blocks[None, :], :].add(
            block_k.transpose(0, 2, 1, 3)
        )
    return lax.psum_scatter(
        totals.reshape(nblocks, rows_mine, nbasis), "grid", scatter_dimension=2, tiled=True
    )


def solution(mesh):
    placed = (
        P(None, "rows", "grid"),
        P("grid", None, "rows", None),
        P("grid", None, None),
        P("grid", None),
        P("grid", None),
    )
    return jax.shard_map(
        body, mesh=mesh, in_specs=placed, out_specs=P(None, "rows", "grid"), check_vma=False
    )
```

profile of v0, /device:TPU:2, one launch (start us, length us, event | category | flops | bytes accessed | tf_op | source)
XLA Modules:
  0.0 494.6 jit_solution(1196830963108560420)
XLA Ops:
  8.6 59.6 %all_to_all.10 = bf16[8,16,16,512]{3,2,1,0:T(8,128)(2,1)} all-to-all(bf16[8,16,16,512]{3,2,1,0:T(8,128)(2,1)S(1)} %broadcast_in_dim.59), channel_id=1, replica_groups=mesh['grid'=32,'rows'=8] {'rows'}, dimensions={0} | all-to-all | bytes 4194304 | tf_op jit(solution)/shard_map/all_to_all | solution.py:9
  69.8 3.7 all-to-all-start
  73.7 3.2 copy.34
  76.8 46.5 %all-to-all-done = bf16[8,16,16,512]{3,2,1,0:T(8,128)(2,1)S(1)} async-done(((bf16[8,16,16,512]{3,2,1,0:T(8,128)(2,1)}), bf16[8,16,16,512]{3,2,1,0:T(8,128)(2,1)S(1)}, u32[]{:S(2)}, u32[]{:S(2)}) %all-to-all-start) | async-done | bytes 2097184 | tf_op jit(solution)/shard_map/all_to_all | solution.py:9
  124.9 2.9 gather_fusion.2
  131.1 2.9 gather_fusion
  137.2 4.1 convolution_bitcast_fusion.2
  141.3 3.3 convolution_bitcast_fusion.3
  146.0 77.3 %all-reduce.3.cloned.1.call-done = (f32[512,512]{0,1:T(8,128)}, f32[512,512]{0,1:T(8,128)}) async-done(((f32[512,512]{0,1:T(8,128)}, f32[512,512]{0,1:T(8,128)}), (f32[512,512]{0,1:T(8,128)}, f32[512,512]{0,1:T(8,128)})) %all-reduce.3.cloned.1.call-update) | async-done | bytes 2097168 | tf_op jit(solution)/shard_map/psum | solution.py:48
  223.3 2.3 fusion
  226.4 2.3 fusion.1
  229.3 36.4 %all-gather.6.cloned.1.call-done = bf16[16,128,512]{2,1,0:T(8,128)(2,1)} async-done(((bf16[16,16,512]{2,1,0:T(8,128)(2,1)}), bf16[16,128,512]{2,1,0:T(8,128)(2,1)}) %all-gather.6.cloned.1.call-update) | async-done | bytes 2097168 | tf_op jit(solution)/shard_map/all_gather | solution.py:61
  265.7 2.3 convolution_bitcast_fusion.1
  268.0 2.0 copy.30
  270.0 2.3 copy.31
  272.2 34.5 %all-gather.8.cloned.1.call-done = bf16[16,128,512]{2,1,0:T(8,128)(2,1)} async-done(((bf16[16,16,512]{2,1,0:T(8,128)(2,1)}), bf16[16,128,512]{2,1,0:T(8,128)(2,1)}) %all-gather.8.cloned.1.call-update) | async-done | bytes 2097168 | tf_op jit(solution)/shard_map/all_gather | solution.py:61
  306.8 3.6 convolution_bitcast_fusion
  310.4 3.1 copy.35
  313.5 3.6 copy.36
  317.1 4.2 broadcast_in_dim.51
  321.3 28.4 %scatter_fusion = f32[32,16,32,128]{3,1,2,0:T(8,128)} fusion(f32[32,16,32,128]{3,1,2,0:T(8,128)} %broadcast_in_dim.51, s32[256]{0:T(256)S(1)} %reshape.140, f32[256,16,128]{2,1,0:T(8,128)S(1)} %bitcast.107), kind=kCustom, calls=%fused_computation.4 | custom fusion | flops 524288 | bytes 6293504 | tf_op jit(solution)/shard_map/scatter-add | solution.py:65
  349.7 31.8 %scatter_fusion.1 = f32[32,16,32,128]{3,1,2,0:T(8,128)} fusion(f32[32,16,32,128]{3,1,2,0:T(8,128)} %scatter_fusion, s32[256]{0:T(256)S(1)} %reshape.146, f32[256,16,128]{2,1,0:T(8,128)} %bitcast.108), kind=kCustom, calls=%fused_computation.5 | custom fusion | flops 524288 | bytes 6293504 | tf_op jit(solution)/shard_map/scatter-add | solution.py:65
  381.5 7.8 %copy_bitcast_fusion = f32[32,16,4096]{2,1,0:T(8,128)} fusion(f32[32,16,32,128]{3,1,2,0:T(8,128)} %scatter_fusion.1), kind=kLoop, calls=%fused_computation.6 | loop fusion | bytes 16777216 | tf_op jit(solution)/shard_map/reshape | solution.py:69
  389.3 98.8 %reduce-scatter.2.cloned.1.call-done = f32[32,16,128]{2,1,0:T(8,128)} async-done(((f32[32,16,4096]{2,1,0:T(8,128)}), f32[32,16,128]{2,1,0:T(8,128)}) %reduce-scatter.2.cloned.1.call-update) | async-done | bytes 262160 | tf_op jit(solution)/shard_map/reduce_scatter | solution.py:68
  (49 shorter events, 14.5 us)
Async XLA Ops:
  6.5 118.4 %all-gather.4.cloned.1.call-start = ((), (), s32[]{:S(2)}) async-start(), calls=%async_computation.3 | async-start | bytes 4325376 | tf_op jit(solution)/shard_map/all_gather | solution.py:30
  69.8 3.8 copy-start.3
  69.8 53.5 %all-to-all-start = ((bf16[8,16,16,512]{3,2,1,0:T(8,128)(2,1)}), bf16[8,16,16,512]{3,2,1,0:T(8,128)(2,1)S(1)}, u32[]{:S(2)}, u32[]{:S(2)}) async-start(bf16[8,16,16,512]{3,2,1,0:T(8,128)(2,1)} %broadcast_in_dim.55), calls=%async_computation | async-start | bytes 4194304 | tf_op jit(solution)/shard_map/all_to_all | solution.py:9
  73.5 149.8 %all-reduce.3.cloned.1.call-start = ((), (), s32[]{:S(2)}) async-start(), calls=%async_computation.7 | async-start | bytes 4194304 | tf_op jit(solution)/shard_map/psum | solution.py:48
  137.2 4.1 copy-start
  144.6 0.7 copy-start.1
  144.6 1.4 copy-start.2
  144.6 121.1 %all-gather.6.cloned.1.call-start = ((), (), s32[]{:S(2)}) async-start(), calls=%async_computation.4 | async-start | bytes 2359296 | tf_op jit(solution)/shard_map/all_gather | solution.py:61
  225.7 81.1 %all-gather.8.cloned.1.call-start = ((), (), s32[]{:S(2)}) async-start(), calls=%async_computation.5 | async-start | bytes 2359296 | tf_op jit(solution)/shard_map/all_gather | solution.py:61
  228.7 259.3 %reduce-scatter.2.cloned.1.call-start = ((), (), s32[]{:S(2)}) async-start(), calls=%async_computation.6 | async-start | bytes 8650752 | tf_op jit(solution)/shard_map/reduce_scatter | solution.py:68
Sparse Core Ops, SparseCore 0:
  9.8 56.2 all-gather.3
  144.7 78.5 all-reduce.2
  225.8 39.8 all-gather.5
  267.3 39.4 all-gather.7
  389.4 98.5 reduce-scatter.1
where the time goes:
time: 496 us; the launch traced here: 495 us
  waiting for transfers between devices  294 us (59%)
  other arithmetic  61.6 us (12%)
  blocking collectives  59.6 us (12%)
  local copies, waits for them, and re-layouts  43.8 us (9%)
  matrix products  17.9 us (4%)
  between operations  13.4 us (3%)
    reduce_scatter x1, waiting for transfers between devices, body(): lax.psum_scatter(totals.reshape(nblocks, rows_mine, nbasis), 'grid', scat...  98.8 us
    psum x1, waiting for transfers between devices, body(): intersection = lax.psum(intersection_part, 'rows')  77.3 us
    all_gather x2, waiting for transfers between devices, body(): lax.all_gather(potential, 'rows', axis=1, tiled=True)  70.9 us
    scatter-add x2, other arithmetic, body(): totals.at[blocks[:, None], :, blocks[None, :], :]  60.2 us
    all_to_all x1, blocking collectives, copy_for_each(): return lax.all_to_all(copies, axis, split_axis=0, concat_axis=0, tiled=True)  59.6 us
    all_to_all x1, waiting for transfers between devices, copy_for_each(): return lax.all_to_all(copies, axis, split_axis=0, concat_axis=0, tiled=True)  46.5 us
  transfers between devices with their start and end apart: 6, of which 5 were waited for; matrix products, arithmetic and copies ran while one was open for 4% of the time, Pallas kernels for 0%

commit v1 on v0

--- a/solution.py
+++ b/solution.py
@@ -2,6 +2,20 @@
 import jax.numpy as jnp
 from jax import lax
 from jax.sharding import PartitionSpec as P
+
+
+def bind_limits(along_axis, message):
+    fan = lax.axis_size(along_axis)
+    samples = [(src_i, (src_i + 1) % fan) for src_i in range(fan)]
+    rows = [(src_i, (src_i - 1) % fan) for src_i in range(fan)]
+    block_now, block_last = ([message], [message])
+    for _ in range(fan // 2):
+        current_arr = lax.ppermute(block_now[-1], along_axis, perm=samples)
+        block_now.append(current_arr)
+    for _ in range((fan - 1) // 2):
+        block_last.append(lax.ppermute(block_last[-1], along_axis, perm=rows))
+    frame_out = jnp.concatenate([*block_now[::-1], *block_last[1:]], axis=1)
+    return jnp.roll(frame_out, (lax.axis_index(along_axis) - fan // 2) * message.shape[1], 1)
 
 
 def copy_for_each(shard, axis):
@@ -58,7 +72,7 @@
         block_k = jnp.einsum(
             "mp,tkp->mtk",
             x_mine,
-            lax.all_gather(potential, "rows", axis=1, tiled=True),
+            bind_limits("rows", potential),
             preferred_element_type=jnp.float32,
         )
         block_k = block_k.reshape(nsig, rows_mine, nsig, block_size)

time: 496 us -> 475 us (0.958)
  waiting for transfers between devices: 294 us -> 247 us
  starting transfers between devices: 4.08 us -> 23.7 us
  local copies, waits for them, and re-layouts: 43.8 us -> 53.5 us
    all_gather x2 -> x0, waiting for transfers between devices: 70.9 us -> none  [body(): lax.all_gather(potential, 'rows', axis=1, tiled=True)]
    ppermute x0 -> x14, waiting for transfers between devices: none -> 24.9 us  [the longest x8 24.5 us: bind_limits(): current_arr = lax.ppermute(block_now[-1], along_axis, perm=samples)]
    ppermute x0 -> x14, starting transfers between devices: none -> 19.9 us  [the longest x6 17.2 us: bind_limits(): block_last.append(lax.ppermute(block_last[-1], along_axis, perm=rows))]
    unnamed x11 -> x41, local copies, waits for them, and re-layouts: 1.59 us -> 9.81 us
  transfers between devices with their start and end apart: 6 -> 18, of which waited for: 5 -> 10; matrix products, arithmetic and copies ran while one was open for 4% -> 5% of each run, Pallas kernels for 0% -> 0%
where the time goes in v1:
time: 475 us; the launch traced here: 474 us
  waiting for transfers between devices  247 us (52%)
  other arithmetic  61.6 us (13%)
  blocking collectives  59.6 us (13%)
  local copies, waits for them, and re-layouts  53.5 us (11%)
  starting transfers between devices  23.7 us (5%)
  matrix products  14.2 us (3%)
  between operations  13.5 us (3%)
    reduce_scatter x1, waiting for transfers between devices, body(): lax.psum_scatter(totals.reshape(nblocks, rows_mine, nbasis), 'grid', scat...  98.8 us
    psum x1, waiting for transfers between devices, body(): intersection = lax.psum(intersection_part, 'rows')  76.6 us
    scatter-add x2, other arithmetic, body(): totals.at[blocks[:, None], :, blocks[None, :], :]  60.2 us
    all_to_all x1, blocking collectives, copy_for_each(): return lax.all_to_all(copies, axis, split_axis=0, concat_axis=0, tiled=True)  59.6 us
    all_to_all x1, waiting for transfers between devices, copy_for_each(): return lax.all_to_all(copies, axis, split_axis=0, concat_axis=0, tiled=True)  46.5 us
    ppermute x8, waiting for transfers between devices, bind_limits(): current_arr = lax.ppermute(block_now[-1], along_axis, perm=samples)  24.5 us
    ppermute x6, starting transfers between devices, bind_limits(): block_last.append(lax.ppermute(block_last[-1], along_axis, perm=rows))  17.2 us
    unnamed x41, local copies, waits for them, and re-layouts  9.81 us
  transfers between devices with their start and end apart: 18, of which 10 were waited for; matrix products, arithmetic and copies ran while one was open for 5% of the time, Pallas kernels for 0%

profile of v1, /device:TPU:2, one launch (start us, length us, event | category | flops | bytes accessed | tf_op | source)
XLA Modules:
  0.0 473.5 jit_solution(90318318561913558)
XLA Ops:
  9.3 59.6 %all_to_all.10 = bf16[8,16,16,512]{3,2,1,0:T(8,128)(2,1)} all-to-all(bf16[8,16,16,512]{3,2,1,0:T(8,128)(2,1)S(1)} %broadcast_in_dim.55), channel_id=1, replica_groups=mesh['grid'=32,'rows'=8] {'rows'}, dimensions={0} | all-to-all | bytes 4194304 | tf_op jit(solution)/shard_map/all_to_all | solution.py:23
  70.5 3.7 all-to-all-start.1
  74.4 3.2 copy.29
  77.6 46.5 %all-to-all-done.1 = bf16[8,16,16,512]{3,2,1,0:T(8,128)(2,1)S(1)} async-done(((bf16[8,16,16,512]{3,2,1,0:T(8,128)(2,1)}), bf16[8,16,16,512]{3,2,1,0:T(8,128)(2,1)S(1)}, u32[]{:S(2)}, u32[]{:S(2)}) %all-to-all-start.1) | async-done | bytes 2097184 | tf_op jit(solution)/shard_map/all_to_all | solution.py:23
  137.0 3.8 convolution_bitcast_fusion.1
  140.8 3.3 convolution_bitcast_fusion
  146.3 76.6 %all-reduce.3.cloned.1.call-done = (f32[512,512]{0,1:T(8,128)}, f32[512,512]{0,1:T(8,128)}) async-done(((f32[512,512]{0,1:T(8,128)}, f32[512,512]{0,1:T(8,128)}), (f32[512,512]{0,1:T(8,128)}, f32[512,512]{0,1:T(8,128)})) %all-reduce.3.cloned.1.call-update) | async-done | bytes 2097168 | tf_op jit(solution)/shard_map/psum | solution.py:62
  227.4 7.3 %collective-permute-done = bf16[16,16,512]{2,1,0:T(8,128)(2,1)S(1)} collective-permute-done((bf16[16,16,512]{2,1,0:T(8,128)(2,1)S(1)}, bf16[16,16,512]{2,1,0:T(8,128)(2,1)S(1)}, u32[]{:S(2)}, u32[]{:S(2)}) %collective-permute-start) | collective-permute-done | bytes 262176 | tf_op jit(solution)/shard_map/ppermute | solution.py:13
  234.8 3.2 collective-permute-start.4
  240.5 5.6 %collective-permute-done.1 = bf16[16,16,512]{2,1,0:T(8,128)(2,1)S(1)} collective-permute-done((bf16[16,16,512]{2,1,0:T(8,128)(2,1)S(1)}, bf16[16,16,512]{2,1,0:T(8,128)(2,1)S(1)}, u32[]{:S(2)}, u32[]{:S(2)}) %collective-permute-start.1) | collective-permute-done | bytes 262176 | tf_op jit(solution)/shard_map/ppermute | solution.py:13
  246.1 3.3 collective-permute-start.5
  249.7 3.7 collective-permute-start.12
  253.4 3.8 collective-permute-done.2
  257.6 3.3 collective-permute-start.6
  260.9 3.8 collective-permute-start.13
  268.9 3.5 collective-permute-done.10
  285.5 3.9 fusion.9
  289.4 3.0 copy.35
  292.4 3.6 copy.36
  296.0 4.2 broadcast_in_dim.51
  300.3 28.4 %scatter_fusion = f32[32,16,32,128]{3,1,2,0:T(8,128)} fusion(f32[32,16,32,128]{3,1,2,0:T(8,128)} %broadcast_in_dim.51, s32[256]{0:T(256)S(1)} %reshape.140, f32[256,16,128]{2,1,0:T(8,128)S(1)} %bitcast.105), kind=kCustom, calls=%fused_computation.4 | custom fusion | flops 524288 | bytes 6293504 | tf_op jit(solution)/shard_map/scatter-add | solution.py:79
  328.7 31.8 %scatter_fusion.1 = f32[32,16,32,128]{3,1,2,0:T(8,128)} fusion(f32[32,16,32,128]{3,1,2,0:T(8,128)} %scatter_fusion, s32[256]{0:T(256)S(1)} %reshape.146, f32[256,16,128]{2,1,0:T(8,128)} %bitcast.106), kind=kCustom, calls=%fused_computation.5 | custom fusion | flops 524288 | bytes 6293504 | tf_op jit(solution)/shard_map/scatter-add | solution.py:79
  360.5 7.7 %copy_bitcast_fusion = f32[32,16,4096]{2,1,0:T(8,128)} fusion(f32[32,16,32,128]{3,1,2,0:T(8,128)} %scatter_fusion.1), kind=kLoop, calls=%fused_computation.6 | loop fusion | bytes 16777216 | tf_op jit(solution)/shard_map/reshape | solution.py:83
  368.3 98.8 %reduce-scatter.2.cloned.1.call-done = f32[32,16,128]{2,1,0:T(8,128)} async-done(((f32[32,16,4096]{2,1,0:T(8,128)}), f32[32,16,128]{2,1,0:T(8,128)}) %reduce-scatter.2.cloned.1.call-update) | async-done | bytes 262160 | tf_op jit(solution)/shard_map/reduce_scatter | solution.py:82
  (103 shorter events, 44.6 us)
Async XLA Ops:
  6.5 119.2 %all-gather.2.cloned.1.call-start = ((), (), s32[]{:S(2)}) async-start(), calls=%async_computation.3 | async-start | bytes 4325376 | tf_op jit(solution)/shard_map/all_gather | solution.py:44
  70.5 53.5 %all-to-all-start.1 = ((bf16[8,16,16,512]{3,2,1,0:T(8,128)(2,1)}), bf16[8,16,16,512]{3,2,1,0:T(8,128)(2,1)S(1)}, u32[]{:S(2)}, u32[]{:S(2)}) async-start(bf16[8,16,16,512]{3,2,1,0:T(8,128)(2,1)} %broadcast_in_dim.59), calls=%async_computation.1 | async-start | bytes 4194304 | tf_op jit(solution)/shard_map/all_to_all | solution.py:23
  74.3 148.5 %all-reduce.3.cloned.1.call-start = ((), (), s32[]{:S(2)}) async-start(), calls=%async_computation.5 | async-start | bytes 4194304 | tf_op jit(solution)/shard_map/psum | solution.py:62
  144.1 322.9 %reduce-scatter.2.cloned.1.call-start = ((), (), s32[]{:S(2)}) async-start(), calls=%async_computation.4 | async-start | bytes 8650752 | tf_op jit(solution)/shard_map/reduce_scatter | solution.py:82
  224.6 10.2 %collective-permute-start = (bf16[16,16,512]{2,1,0:T(8,128)(2,1)S(1)}, bf16[16,16,512]{2,1,0:T(8,128)(2,1)S(1)}, u32[]{:S(2)}, u32[]{:S(2)}) collective-permute-start(bf16[16,16,512]{2,1,0:T(8,128)(2,1)S(1)} %bitcast.118), channel_id=1, source_target_pairs={{0,1},{1,2},{2,3},{3,4},{4,5},{5,6},{6,7},{7,0},{8,9},{9,10},{10,1... | collective-permute-start | bytes 786440 | tf_op jit(solution)/shard_map/ppermute | solution.py:13
  226.0 14.4 %collective-permute-start.7 = (bf16[16,16,512]{2,1,0:T(8,128)(2,1)S(1)}, bf16[16,16,512]{2,1,0:T(8,128)(2,1)S(1)}, u32[]{:S(2)}, u32[]{:S(2)}) collective-permute-start(bf16[16,16,512]{2,1,0:T(8,128)(2,1)S(1)} %bitcast.115), channel_id=1, source_target_pairs={{0,1},{1,2},{2,3},{3,4},{4,5},{5,6},{6,7},{7,0},{8,9},{9,10},{10,1... | collective-permute-start | bytes 786440 | tf_op jit(solution)/shard_map/ppermute | solution.py:13
  234.8 11.2 %collective-permute-start.1 = (bf16[16,16,512]{2,1,0:T(8,128)(2,1)S(1)}, bf16[16,16,512]{2,1,0:T(8,128)(2,1)S(1)}, u32[]{:S(2)}, u32[]{:S(2)}) collective-permute-start(bf16[16,16,512]{2,1,0:T(8,128)(2,1)S(1)} %collective-permute-done), channel_id=1, source_target_pairs={{0,1},{1,2},{2,3},{3,4},{4,5},{5,6},{6,7},{7,0},{8,9},{9,10},{10,1... | collective-permute-start | bytes 786440 | tf_op jit(solution)/shard_map/ppermute | solution.py:13
  234.8 11.3 %collective-permute-start.4 = (bf16[16,16,512]{2,1,0:T(8,128)(2,1)S(1)}, bf16[16,16,512]{2,1,0:T(8,128)(2,1)S(1)}, u32[]{:S(2)}, u32[]{:S(2)}) collective-permute-start(bf16[16,16,512]{2,1,0:T(8,128)(2,1)S(1)} %bitcast.119), channel_id=1, source_target_pairs={{0,7},{1,0},{2,1},{3,2},{4,3},{5,4},{6,5},{7,6},{8,15},{9,8},{10,9... | collective-permute-start | bytes 786440 | tf_op jit(solution)/shard_map/ppermute | solution.py:16
  238.0 11.7 %collective-permute-start.11 = (bf16[16,16,512]{2,1,0:T(8,128)(2,1)S(1)}, bf16[16,16,512]{2,1,0:T(8,128)(2,1)S(1)}, u32[]{:S(2)}, u32[]{:S(2)}) collective-permute-start(bf16[16,16,512]{2,1,0:T(8,128)(2,1)S(1)} %bitcast.116), channel_id=1, source_target_pairs={{0,7},{1,0},{2,1},{3,2},{4,3},{5,4},{6,5},{7,6},{8,15},{9,8},{10,9... | collective-permute-start | bytes 786440 | tf_op jit(solution)/shard_map/ppermute | solution.py:16
  240.4 17.2 %copy-start.3 = (bf16[16,16,512]{2,1,0:T(8,128)(2,1)}, bf16[16,16,512]{2,1,0:T(8,128)(2,1)S(1)}, u32[]{:S(2)}) copy-start(bf16[16,16,512]{2,1,0:T(8,128)(2,1)S(1)} %collective-permute-done.7) | copy-start | bytes 786436
  240.4 13.0 %collective-permute-start.8 = (bf16[16,16,512]{2,1,0:T(8,128)(2,1)S(1)}, bf16[16,16,512]{2,1,0:T(8,128)(2,1)S(1)}, u32[]{:S(2)}, u32[]{:S(2)}) collective-permute-start(bf16[16,16,512]{2,1,0:T(8,128)(2,1)S(1)} %collective-permute-done.7), channel_id=1, source_target_pairs={{0,1},{1,2},{2,3},{3,4},{4,5},{5,6},{6,7},{7,0},{8,9},{9,10},{10,1... | collective-permute-start | bytes 786440 | tf_op jit(solution)/shard_map/ppermute | solution.py:13
  246.0 11.2 %collective-permute-start.2 = (bf16[16,16,512]{2,1,0:T(8,128)(2,1)S(1)}, bf16[16,16,512]{2,1,0:T(8,128)(2,1)S(1)}, u32[]{:S(2)}, u32[]{:S(2)}) collective-permute-start(bf16[16,16,512]{2,1,0:T(8,128)(2,1)S(1)} %collective-permute-done.1), channel_id=1, source_target_pairs={{0,1},{1,2},{2,3},{3,4},{4,5},{5,6},{6,7},{7,0},{8,9},{9,10},{10,1... | collective-permute-start | bytes 786440 | tf_op jit(solution)/shard_map/ppermute | solution.py:13
  246.1 11.5 %collective-permute-start.5 = (bf16[16,16,512]{2,1,0:T(8,128)(2,1)S(1)}, bf16[16,16,512]{2,1,0:T(8,128)(2,1)S(1)}, u32[]{:S(2)}, u32[]{:S(2)}) collective-permute-start(bf16[16,16,512]{2,1,0:T(8,128)(2,1)S(1)} %collective-permute-done.4), channel_id=1, source_target_pairs={{0,7},{1,0},{2,1},{3,2},{4,3},{5,4},{6,5},{7,6},{8,15},{9,8},{10,9... | collective-permute-start | bytes 786440 | tf_op jit(solution)/shard_map/ppermute | solution.py:16
  249.7 18.0 %copy-start.5 = (bf16[16,16,512]{2,1,0:T(8,128)(2,1)}, bf16[16,16,512]{2,1,0:T(8,128)(2,1)S(1)}, u32[]{:S(2)}) copy-start(bf16[16,16,512]{2,1,0:T(8,128)(2,1)S(1)} %collective-permute-done.11) | copy-start | bytes 786436
  249.7 11.2 %collective-permute-start.12 = (bf16[16,16,512]{2,1,0:T(8,128)(2,1)S(1)}, bf16[16,16,512]{2,1,0:T(8,128)(2,1)}, u32[]{:S(2)}, u32[]{:S(2)}) collective-permute-start(bf16[16,16,512]{2,1,0:T(8,128)(2,1)S(1)} %collective-permute-done.11), channel_id=1, source_target_pairs={{0,7},{1,0},{2,1},{3,2},{4,3},{5,4},{6,5},{7,6},{8,15},{9,8},{10,9... | collective-permute-start | bytes 786440 | tf_op jit(solution)/shard_map/ppermute | solution.py:16
  253.4 14.3 %copy-start.7 = (bf16[16,16,512]{2,1,0:T(8,128)(2,1)}, bf16[16,16,512]{2,1,0:T(8,128)(2,1)S(1)}, u32[]{:S(2)}) copy-start(bf16[16,16,512]{2,1,0:T(8,128)(2,1)S(1)} %collective-permute-done.8) | copy-start | bytes 786436
  253.4 11.2 %collective-permute-start.9 = (bf16[16,16,512]{2,1,0:T(8,128)(2,1)S(1)}, bf16[16,16,512]{2,1,0:T(8,128)(2,1)}, u32[]{:S(2)}, u32[]{:S(2)}) collective-permute-start(bf16[16,16,512]{2,1,0:T(8,128)(2,1)S(1)} %collective-permute-done.8), channel_id=1, source_target_pairs={{0,1},{1,2},{2,3},{3,4},{4,5},{5,6},{6,7},{7,0},{8,9},{9,10},{10,1... | collective-permute-start | bytes 786440 | tf_op jit(solution)/shard_map/ppermute | solution.py:13
  257.2 9.3 %collective-permute-start.3 = (bf16[16,16,512]{2,1,0:T(8,128)(2,1)S(1)}, bf16[16,16,512]{2,1,0:T(8,128)(2,1)}, u32[]{:S(2)}, u32[]{:S(2)}) collective-permute-start(bf16[16,16,512]{2,1,0:T(8,128)(2,1)S(1)} %collective-permute-done.2), channel_id=1, source_target_pairs={{0,1},{1,2},{2,3},{3,4},{4,5},{5,6},{6,7},{7,0},{8,9},{9,10},{10,1... | collective-permute-start | bytes 786440 | tf_op jit(solution)/shard_map/ppermute | solution.py:13
  257.6 10.2 %copy-start.2 = (bf16[1,16,16,512]{3,2,1,0:T(8,128)(2,1)S(1)}, bf16[1,16,16,512]{3,2,1,0:T(8,128)(2,1)}, u32[]{:S(2)}) copy-start(bf16[1,16,16,512]{3,2,1,0:T(8,128)(2,1)} %get-tuple-element.17) | copy-start | bytes 786436
  257.6 10.1 %collective-permute-start.6 = (bf16[16,16,512]{2,1,0:T(8,128)(2,1)S(1)}, bf16[16,16,512]{2,1,0:T(8,128)(2,1)S(1)}, u32[]{:S(2)}, u32[]{:S(2)}) collective-permute-start(bf16[16,16,512]{2,1,0:T(8,128)(2,1)S(1)} %collective-permute-done.5), channel_id=1, source_target_pairs={{0,7},{1,0},{2,1},{3,2},{4,3},{5,4},{6,5},{7,6},{8,15},{9,8},{10,9... | collective-permute-start | bytes 786440 | tf_op jit(solution)/shard_map/ppermute | solution.py:16
  260.9 22.9 %collective-permute-start.13 = (bf16[16,16,512]{2,1,0:T(8,128)(2,1)}, bf16[16,16,512]{2,1,0:T(8,128)(2,1)}, u32[]{:S(2)}, u32[]{:S(2)}) collective-permute-start(bf16[16,16,512]{2,1,0:T(8,128)(2,1)} %collective-permute-done.12), channel_id=1, source_target_pairs={{0,7},{1,0},{2,1},{3,2},{4,3},{5,4},{6,5},{7,6},{8,15},{9,8},{10,9... | collective-permute-start | bytes 786440 | tf_op jit(solution)/shard_map/ppermute | solution.py:16
  264.7 7.8 %collective-permute-start.10 = (bf16[16,16,512]{2,1,0:T(8,128)(2,1)}, bf16[16,16,512]{2,1,0:T(8,128)(2,1)S(1)}, u32[]{:S(2)}, u32[]{:S(2)}) collective-permute-start(bf16[16,16,512]{2,1,0:T(8,128)(2,1)} %collective-permute-done.9), channel_id=1, source_target_pairs={{0,1},{1,2},{2,3},{3,4},{4,5},{5,6},{6,7},{7,0},{8,9},{9,10},{10,1... | collective-permute-start | bytes 786440 | tf_op jit(solution)/shard_map/ppermute | solution.py:13
  267.8 7.1 %copy-start.8 = (bf16[16,16,512]{2,1,0:T(8,128)(2,1)S(1)}, bf16[16,16,512]{2,1,0:T(8,128)(2,1)}, u32[]{:S(2)}) copy-start(bf16[16,16,512]{2,1,0:T(8,128)(2,1)} %copy-done.7) | copy-start | bytes 786436
  267.8 7.8 %copy-start.4 = (bf16[16,16,512]{2,1,0:T(8,128)(2,1)S(1)}, bf16[16,16,512]{2,1,0:T(8,128)(2,1)}, u32[]{:S(2)}) copy-start(bf16[16,16,512]{2,1,0:T(8,128)(2,1)} %copy-done.3) | copy-start | bytes 786436
  (6 other events, 14.2 us)
Sparse Core Ops, SparseCore 0:
  9.8 56.2 all-gather.1
  144.2 78.5 all-reduce.2
  368.4 98.5 reduce-scatter.1
